TPU v7x, 128 devices: a whole 4x4x4 slice. The times are simulated.
128 devices in a mesh: area: 32 (over z, y, core), local: 4 (over x).
Axes of the slice: x: 4, y: 4, z: 4, core: 2. Of those that a mesh axis runs over, the one named last changes fastest.
Arguments:
- potential: float32 [8, 524288], P(None, ('area', 'local')), may hold values from -6 to 6
- current: float32 [8, 524288], P(None, ('area', 'local')), may hold values from -4 to 4
- ext_drive: float32 [8, 524288], P(None, ('area', 'local')), may hold values from -6 to 6
- decay_syn: float32 [524288], P(('area', 'local')), may hold values from 0.3 to 0.97
- decay_mem: float32 [524288], P(('area', 'local')), may hold values from 0.4 to 0.95
- weights: bfloat16 [128, 128, 2, 128, 128], P(('area', 'local')), may hold values from -0.25 to 0.25
- tile_src: int32 [128, 128, 2], P(('area', 'local')), may hold values from 0 to 31
- tile_dst: int32 [128, 128, 2], P(('area', 'local')), may hold values from 0 to 31
- blk_pop: int32 [4096], P(('area', 'local')), may hold values from 0 to 7
- tile_route: int32 [5, 128, 128, 1], P(None, ('area', 'local')), may hold values from 0 to 1, as said below
- counts: int32 [5, 128, 128], P(None, ('area', 'local')), may hold values from 0 to 1, as said below
Outputs:
- volts_out: float32 [8, 524288], P(None, ('area', 'local'))
- current_out: float32 [8, 524288], P(None, ('area', 'local'))
- pop_rates: float32 [32, 5, 8, 8], P('area')
Inputs may be any that keep to these rules, and one draw needn't show every extreme that they name: `tile_route`: the 1 entries of one list name distinct tiles; entries at and beyond counts of that list are unused. `counts`: in every step some target device gets 1 tiles from every sending device.
All inputs are finite; a program needn't handle non-finite values.
Results may differ from a plain program's by a relative error of at most 0.0029.
Values may be sent and summed in bfloat16 or wider, within the bound.
No kernel may reach another device: no remote copies, remote signals or barrier semaphores. Data moves between devices by JAX's collectives and lax.ppermute only.
A program may use at most 64 MiB of HBM per device.

v0:
```python
import jax
import jax.numpy as jnp
from jax import lax
from jax.sharding import PartitionSpec as P

POPS = 8
spike_gain = 4.0
threshold = 1.0
reset_size = 0.5


def from_everyone(array, axis):
    copies = jnp.broadcast_to(array, (lax.axis_size(axis), *array.shape))
    return lax.all_to_all(copies, axis, split_axis=0, concat_axis=0, tiled=True)


def of_everyone(array, axis):
    return from_everyone(array, axis).sum(axis=0)


def shards(
    potential,
    current,
    ext_drive,
    decay_syn,
    decay_mem,
    weights,
    tile_src,
    tile_dst,
    blk_pop,
    tile_route,
    counts,
):
    dev_count = weights.shape[1]
    tile_count = weights.shape[2]
    block_width = weights.shape[3]
    blk_count = blk_pop.shape[0]
    trial_count = potential.shape[0]
    slot_count = tile_route.shape[3]
    step_count = tile_route.shape[0]
    tile_table = weights[0]
    routes = tile_route[:, 0]
    slot_valid = jnp.arange(slot_count, dtype=jnp.int32)[None, None, :] < counts[:, 0][:, :, None]
    table_shape = (step_count, dev_count, tile_count)
    src_blocks = jnp.take_along_axis(
        jnp.broadcast_to(tile_src[0][None], table_shape), routes, axis=2
    )
    dst_blocks = jnp.take_along_axis(
        jnp.broadcast_to(tile_dst[0][None], table_shape), routes, axis=2
    )
    dst_ids = jnp.where(slot_valid, dst_blocks, -1)
    arrived_ids = lax.all_to_all(
        dst_ids, ("area", "local"), split_axis=1, concat_axis=1, tiled=True
    )
    state_shape = (trial_count, blk_count, block_width)
    volts = potential.reshape(state_shape)
    syn_cur = current.reshape(state_shape)
    ext_field = ext_drive.reshape(state_shape)
    syn_decay = decay_syn.reshape((1, blk_count, block_width))
    mem_decay = decay_mem.reshape((1, blk_count, block_width))
    pop_table = (blk_pop[:, None] == jnp.arange(POPS, dtype=jnp.int32)[None, :]).astype(jnp.float32)
    block_ids = jnp.arange(blk_count, dtype=jnp.int32)

    def advance(step_idx, state_now):
        volts, syn_cur, rate_acc = state_now
        spikes = jax.nn.sigmoid(spike_gain * (volts - threshold))
        spike_blocks = jnp.transpose(spikes.astype(jnp.bfloat16), (1, 0, 2))
        activity = jnp.sum(spikes, axis=2)
        rate_now = jnp.dot(activity, pop_table, precision=lax.Precision.HIGHEST)
        rate_acc = lax.dynamic_update_index_in_dim(rate_acc, rate_now, step_idx, 0)
        chosen = routes[step_idx]
        picked = jnp.take_along_axis(tile_table, chosen[:, :, None, None], axis=1)
        senders = jnp.take(spike_blocks, src_blocks[step_idx], axis=0)
        outgoing = jnp.einsum(
            "tcrn,tcnm->tcrm", senders, picked, preferred_element_type=jnp.float32
        ).astype(jnp.bfloat16)
        arrived = lax.all_to_all(
            outgoing, ("area", "local"), split_axis=0, concat_axis=0, tiled=True
        )
        targets = arrived_ids[step_idx].reshape((dev_count * slot_count,))
        deliver = (targets[:, None] == block_ids[None, :]).astype(jnp.bfloat16)
        inflow = jnp.einsum(
            "sb,srn->rbn",
            deliver,
            arrived.reshape((dev_count * slot_count, trial_count, block_width)),
            preferred_element_type=jnp.float32,
        )
        syn_cur = syn_decay * syn_cur + inflow
        volts = mem_decay * volts + (1.0 - mem_decay) * (syn_cur + ext_field) - reset_size * spikes
        return (volts, syn_cur, rate_acc)

    rate_start = jnp.zeros((step_count, trial_count, POPS), jnp.float32)
    volts, syn_cur, rate_acc = lax.fori_loop(0, step_count, advance, (volts, syn_cur, rate_start))
    totals = of_everyone(rate_acc, "local") / (block_width * blk_count)
    return (volts.reshape((trial_count, -1)), syn_cur.reshape((trial_count, -1)), totals[None])


def solution(mesh):
    in_specs = (
        P(None, ("area", "local")),
        P(None, ("area", "local")),
        P(None, ("area", "local")),
        P(("area", "local")),
        P(("area", "local")),
        P(("area", "local"), None, None, None, None),
        P(("area", "local"), None, None),
        P(("area", "local"), None, None),
        P(("area", "local")),
        P(None, ("area", "local"), None, None),
        P(None, ("area", "local"), None),
    )
    out_specs = (
        P(None, ("area", "local")),
        P(None, ("area", "local")),
        P("area", None, None, None),
    )
    return jax.shard_map(shards, mesh=mesh, in_specs=in_specs, out_specs=out_specs, check_vma=False)
```

profile of v0, /device:TPU:0, one launch (start us, length us, event | category | flops | bytes accessed | tf_op | source)
XLA Modules:
  0.0 181.6 jit_solution(10345220873550262598)
XLA Ops:
  0.6 0.7 fusion.37
  1.4 0.8 copy.54
  2.2 0.0 copy-start.2
  2.3 0.0 copy-start.3
  2.3 0.0 copy-start.7
  2.3 5.6 %gather_fusion.2 = s32[640]{0:T(1024)S(1)} fusion(s32[5,128,2]{2,1,0:T(8,128)S(1)} %broadcast_in_dim.74, s32[640]{0:T(1024)S(1)} %bitcast.118), kind=kCustom, calls=%fused_computation.clone | custom fusion | bytes 12800 | tf_op jit(solution)/shard_map/jit(take_along_axis)/gather | solution.py:45
  8.0 0.1 copy.56
  8.1 5.6 %gather_fusion.3 = s32[640]{0:T(1024)S(1)} fusion(s32[5,128,2]{2,1,0:T(8,128)S(1)} %broadcast_in_dim.76, s32[640]{0:T(1024)S(1)} %bitcast.119), kind=kCustom, calls=%fused_computation.3.clone | custom fusion | bytes 12800 | tf_op jit(solution)/shard_map/jit(take_along_axis)/gather | solution.py:48
  13.8 0.7 copy.58
  14.6 11.2 %all-to-all-start.1 = ((s32[5,128,1]{0,2,1:T(1,128)}), s32[5,128,1]{0,2,1:T(1,128)S(1)}, u32[]{:S(2)}, u32[]{:S(2)}) async-start(s32[5,128,1]{0,2,1:T(1,128)} %copy.58), calls=%async_computation.1 | async-start | bytes 131072 | tf_op jit(solution)/shard_map/all_to_all | solution.py:52
  25.8 0.1 copy_bitcast_fusion.2
  25.9 9.1 %all-to-all-done.1 = s32[5,128,1]{0,2,1:T(1,128)S(1)} async-done(((s32[5,128,1]{0,2,1:T(1,128)}), s32[5,128,1]{0,2,1:T(1,128)S(1)}, u32[]{:S(2)}, u32[]{:S(2)}) %all-to-all-start.1) | async-done | bytes 2592 | tf_op jit(solution)/shard_map/all_to_all | solution.py:52
  35.0 0.1 copy.59
  35.1 0.0 copy-done.8
  35.1 135.4 %while.20 = (s32[]{:T(128)}, f32[8,32,128]{2,1,0:T(8,128)S(1)}, f32[8,32,128]{2,1,0:T(8,128)S(1)}, f32[5,8,8]{2,1,0:T(8,128)S(1)}, f32[1,32,128]{2,1,0:T(8,128)S...) while((s32[]{:T(128)}, f32[8,32,128]{2,1,0:T(8,128)S(1)}, ...), condition=%wide.region_2.0_spmd.clone, body=%wide.region_0.3_spmd.clone.sunk | while | flops 44994944 | bytes 15770289 | solution.py:93
  35.2 0.1 fusion.53
  35.4 0.7 gather_fusion.1
  36.1 6.5 %gather_fusion = bf16[128,128,128]{2,1,0:T(8,128)(2,1)} fusion(bf16[128,2,128,128]{3,2,1,0:T(8,128)(2,1)} %get-tuple-element.546, s32[128]{0:T(128)S(1)} %or_bitcast_fusion.2), kind=kCustom, calls=%fused_computation.2.clone.clone.1 | custom fusion | bytes 8389632 | tf_op jit(solution)/shard_map/while/body/eval_jaxpr/jit(take_along_axis)/gather | solution.py:72
  42.5 4.2 %fusion.55 = bf16[128,1,8,128]{3,2,1,0:T(8,128)(2,1)} fusion(bf16[128,128,128]{2,1,0:T(8,128)(2,1)} %gather_fusion, pred[128]{0:T(512)(128)(4,1)S(1)} %get-tuple-element.506, bf16[128,8,128]{2,1,0:T(8,128)(2,1)S(1)} %gather_fusion.1, pred[128]{0:T(512)(128)(4,1)S(1)} %get-tuple-element.508), kind=kOutput, calls=%fused_computation.11.clone.1 | convolution fusion | flops 35913728 | bytes 4718848 | tf_op jit(solution)/shard_map/while/body/eval_jaxpr/tcrn,tcnm->tcrm/dot_general | solution.py:74
  46.7 4.6 %all-to-all-start = ((bf16[128,1,8,128]{3,2,1,0:T(8,128)(2,1)}), bf16[128,1,8,128]{3,2,1,0:T(8,128)(2,1)S(1)}, u32[]{:S(2)}, u32[]{:S(2)}) async-start(bf16[128,1,8,128]{3,2,1,0:T(8,128)(2,1)} %fusion.55), calls=%async_computation | async-start | bytes 524288 | tf_op jit(solution)/shard_map/while/body/eval_jaxpr/all_to_all | solution.py:77
  51.3 0.2 fusion.56
  51.5 10.4 %all-to-all-done = bf16[128,1,8,128]{3,2,1,0:T(8,128)(2,1)S(1)} async-done(((bf16[128,1,8,128]{3,2,1,0:T(8,128)(2,1)}), bf16[128,1,8,128]{3,2,1,0:T(8,128)(2,1)S(1)}, u32[]{:S(2)}, u32[]{:S(2)}) %all-to-all-start) | async-done | bytes 262176 | tf_op jit(solution)/shard_map/while/body/eval_jaxpr/all_to_all | solution.py:77
  62.0 0.2 multiply_subtract_fusion.2
  62.3 0.1 fusion.53
  62.5 0.7 gather_fusion.1
  63.2 6.5 %gather_fusion = bf16[128,128,128]{2,1,0:T(8,128)(2,1)} fusion(bf16[128,2,128,128]{3,2,1,0:T(8,128)(2,1)} %get-tuple-element.546, s32[128]{0:T(128)S(1)} %or_bitcast_fusion.2), kind=kCustom, calls=%fused_computation.2.clone.clone.1 | custom fusion | bytes 8389632 | tf_op jit(solution)/shard_map/while/body/eval_jaxpr/jit(take_along_axis)/gather | solution.py:72
  69.6 4.2 %fusion.55 = bf16[128,1,8,128]{3,2,1,0:T(8,128)(2,1)} fusion(bf16[128,128,128]{2,1,0:T(8,128)(2,1)} %gather_fusion, pred[128]{0:T(512)(128)(4,1)S(1)} %get-tuple-element.506, bf16[128,8,128]{2,1,0:T(8,128)(2,1)S(1)} %gather_fusion.1, pred[128]{0:T(512)(128)(4,1)S(1)} %get-tuple-element.508), kind=kOutput, calls=%fused_computation.11.clone.1 | convolution fusion | flops 35913728 | bytes 4718848 | tf_op jit(solution)/shard_map/while/body/eval_jaxpr/tcrn,tcnm->tcrm/dot_general | solution.py:74
  73.8 4.6 %all-to-all-start = ((bf16[128,1,8,128]{3,2,1,0:T(8,128)(2,1)}), bf16[128,1,8,128]{3,2,1,0:T(8,128)(2,1)S(1)}, u32[]{:S(2)}, u32[]{:S(2)}) async-start(bf16[128,1,8,128]{3,2,1,0:T(8,128)(2,1)} %fusion.55), calls=%async_computation | async-start | bytes 524288 | tf_op jit(solution)/shard_map/while/body/eval_jaxpr/all_to_all | solution.py:77
  78.4 0.2 fusion.56
  78.6 10.4 %all-to-all-done = bf16[128,1,8,128]{3,2,1,0:T(8,128)(2,1)S(1)} async-done(((bf16[128,1,8,128]{3,2,1,0:T(8,128)(2,1)}), bf16[128,1,8,128]{3,2,1,0:T(8,128)(2,1)S(1)}, u32[]{:S(2)}, u32[]{:S(2)}) %all-to-all-start) | async-done | bytes 262176 | tf_op jit(solution)/shard_map/while/body/eval_jaxpr/all_to_all | solution.py:77
  89.1 0.2 multiply_subtract_fusion.2
  89.3 0.1 fusion.53
  89.5 0.7 gather_fusion.1
  90.2 6.5 %gather_fusion = bf16[128,128,128]{2,1,0:T(8,128)(2,1)} fusion(bf16[128,2,128,128]{3,2,1,0:T(8,128)(2,1)} %get-tuple-element.546, s32[128]{0:T(128)S(1)} %or_bitcast_fusion.2), kind=kCustom, calls=%fused_computation.2.clone.clone.1 | custom fusion | bytes 8389632 | tf_op jit(solution)/shard_map/while/body/eval_jaxpr/jit(take_along_axis)/gather | solution.py:72
  96.7 4.2 %fusion.55 = bf16[128,1,8,128]{3,2,1,0:T(8,128)(2,1)} fusion(bf16[128,128,128]{2,1,0:T(8,128)(2,1)} %gather_fusion, pred[128]{0:T(512)(128)(4,1)S(1)} %get-tuple-element.506, bf16[128,8,128]{2,1,0:T(8,128)(2,1)S(1)} %gather_fusion.1, pred[128]{0:T(512)(128)(4,1)S(1)} %get-tuple-element.508), kind=kOutput, calls=%fused_computation.11.clone.1 | convolution fusion | flops 35913728 | bytes 4718848 | tf_op jit(solution)/shard_map/while/body/eval_jaxpr/tcrn,tcnm->tcrm/dot_general | solution.py:74
  100.8 4.6 %all-to-all-start = ((bf16[128,1,8,128]{3,2,1,0:T(8,128)(2,1)}), bf16[128,1,8,128]{3,2,1,0:T(8,128)(2,1)S(1)}, u32[]{:S(2)}, u32[]{:S(2)}) async-start(bf16[128,1,8,128]{3,2,1,0:T(8,128)(2,1)} %fusion.55), calls=%async_computation | async-start | bytes 524288 | tf_op jit(solution)/shard_map/while/body/eval_jaxpr/all_to_all | solution.py:77
  105.5 0.2 fusion.56
  105.7 10.4 %all-to-all-done = bf16[128,1,8,128]{3,2,1,0:T(8,128)(2,1)S(1)} async-done(((bf16[128,1,8,128]{3,2,1,0:T(8,128)(2,1)}), bf16[128,1,8,128]{3,2,1,0:T(8,128)(2,1)S(1)}, u32[]{:S(2)}, u32[]{:S(2)}) %all-to-all-start) | async-done | bytes 262176 | tf_op jit(solution)/shard_map/while/body/eval_jaxpr/all_to_all | solution.py:77
  116.1 0.2 multiply_subtract_fusion.2
  116.4 0.1 fusion.53
  116.6 0.7 gather_fusion.1
  117.3 6.5 %gather_fusion = bf16[128,128,128]{2,1,0:T(8,128)(2,1)} fusion(bf16[128,2,128,128]{3,2,1,0:T(8,128)(2,1)} %get-tuple-element.546, s32[128]{0:T(128)S(1)} %or_bitcast_fusion.2), kind=kCustom, calls=%fused_computation.2.clone.clone.1 | custom fusion | bytes 8389632 | tf_op jit(solution)/shard_map/while/body/eval_jaxpr/jit(take_along_axis)/gather | solution.py:72
  123.7 4.2 %fusion.55 = bf16[128,1,8,128]{3,2,1,0:T(8,128)(2,1)} fusion(bf16[128,128,128]{2,1,0:T(8,128)(2,1)} %gather_fusion, pred[128]{0:T(512)(128)(4,1)S(1)} %get-tuple-element.506, bf16[128,8,128]{2,1,0:T(8,128)(2,1)S(1)} %gather_fusion.1, pred[128]{0:T(512)(128)(4,1)S(1)} %get-tuple-element.508), kind=kOutput, calls=%fused_computation.11.clone.1 | convolution fusion | flops 35913728 | bytes 4718848 | tf_op jit(solution)/shard_map/while/body/eval_jaxpr/tcrn,tcnm->tcrm/dot_general | solution.py:74
  127.9 4.6 %all-to-all-start = ((bf16[128,1,8,128]{3,2,1,0:T(8,128)(2,1)}), bf16[128,1,8,128]{3,2,1,0:T(8,128)(2,1)S(1)}, u32[]{:S(2)}, u32[]{:S(2)}) async-start(bf16[128,1,8,128]{3,2,1,0:T(8,128)(2,1)} %fusion.55), calls=%async_computation | async-start | bytes 524288 | tf_op jit(solution)/shard_map/while/body/eval_jaxpr/all_to_all | solution.py:77
  132.5 0.2 fusion.56
  132.7 10.4 %all-to-all-done = bf16[128,1,8,128]{3,2,1,0:T(8,128)(2,1)S(1)} async-done(((bf16[128,1,8,128]{3,2,1,0:T(8,128)(2,1)}), bf16[128,1,8,128]{3,2,1,0:T(8,128)(2,1)S(1)}, u32[]{:S(2)}, u32[]{:S(2)}) %all-to-all-start) | async-done | bytes 262176 | tf_op jit(solution)/shard_map/while/body/eval_jaxpr/all_to_all | solution.py:77
  143.2 0.2 multiply_subtract_fusion.2
  143.5 0.1 fusion.53
  143.7 0.7 gather_fusion.1
  144.4 6.5 %gather_fusion = bf16[128,128,128]{2,1,0:T(8,128)(2,1)} fusion(bf16[128,2,128,128]{3,2,1,0:T(8,128)(2,1)} %get-tuple-element.546, s32[128]{0:T(128)S(1)} %or_bitcast_fusion.2), kind=kCustom, calls=%fused_computation.2.clone.clone.1 | custom fusion | bytes 8389632 | tf_op jit(solution)/shard_map/while/body/eval_jaxpr/jit(take_along_axis)/gather | solution.py:72
  150.8 4.2 %fusion.55 = bf16[128,1,8,128]{3,2,1,0:T(8,128)(2,1)} fusion(bf16[128,128,128]{2,1,0:T(8,128)(2,1)} %gather_fusion, pred[128]{0:T(512)(128)(4,1)S(1)} %get-tuple-element.506, bf16[128,8,128]{2,1,0:T(8,128)(2,1)S(1)} %gather_fusion.1, pred[128]{0:T(512)(128)(4,1)S(1)} %get-tuple-element.508), kind=kOutput, calls=%fused_computation.11.clone.1 | convolution fusion | flops 35913728 | bytes 4718848 | tf_op jit(solution)/shard_map/while/body/eval_jaxpr/tcrn,tcnm->tcrm/dot_general | solution.py:74
  155.0 4.6 %all-to-all-start = ((bf16[128,1,8,128]{3,2,1,0:T(8,128)(2,1)}), bf16[128,1,8,128]{3,2,1,0:T(8,128)(2,1)S(1)}, u32[]{:S(2)}, u32[]{:S(2)}) async-start(bf16[128,1,8,128]{3,2,1,0:T(8,128)(2,1)} %fusion.55), calls=%async_computation | async-start | bytes 524288 | tf_op jit(solution)/shard_map/while/body/eval_jaxpr/all_to_all | solution.py:77
  159.6 0.2 fusion.56
  159.8 10.4 %all-to-all-done = bf16[128,1,8,128]{3,2,1,0:T(8,128)(2,1)S(1)} async-done(((bf16[128,1,8,128]{3,2,1,0:T(8,128)(2,1)}), bf16[128,1,8,128]{3,2,1,0:T(8,128)(2,1)S(1)}, u32[]{:S(2)}, u32[]{:S(2)}) %all-to-all-start) | async-done | bytes 262176 | tf_op jit(solution)/shard_map/while/body/eval_jaxpr/all_to_all | solution.py:77
  170.3 0.2 multiply_subtract_fusion.2
  170.5 0.7 reshape.391
  171.2 3.2 %all-to-all-start.2 = ((f32[4,1,320]{2,1,0:T(1,128)}), f32[4,1,320]{2,1,0:T(1,128)S(1)}, u32[]{:S(2)}, u32[]{:S(2)}) async-start(f32[4,1,320]{2,1,0:T(1,128)} %reshape.391), calls=%async_computation.2 | async-start | bytes 12288 | tf_op jit(solution)/shard_map/all_to_all | solution.py:14
  174.4 0.7 copy.82
  175.2 0.7 copy.83
  175.9 3.8 %all-to-all-done.2 = f32[4,1,320]{2,1,0:T(1,128)S(1)} async-done(((f32[4,1,320]{2,1,0:T(1,128)}), f32[4,1,320]{2,1,0:T(1,128)S(1)}, u32[]{:S(2)}, u32[]{:S(2)}) %all-to-all-start.2) | async-done | bytes 5152 | tf_op jit(solution)/shard_map/all_to_all | solution.py:14
  179.7 0.5 broadcast.389
  180.2 0.7 reduce.2
  180.9 0.1 reshape.392
  181.0 0.6 multiply_bitcast_fusion
  (79 shorter events, 0.7 us)
Async XLA Ops:
  0.6 7.3 %copy-start.6 = (s32[1,128,2]{1,2,0:T(2,128)S(1)}, s32[1,128,2]{1,2,0:T(2,128)}, u32[]{:S(2)}) copy-start(s32[1,128,2]{1,2,0:T(2,128)} %param.22) | copy-start | bytes 3076
  2.2 11.5 %copy-start.5 = (s32[5,1,128]{2,1,0:T(1,128)S(1)}, s32[5,1,128]{2,1,0:T(1,128)}, u32[]{:S(2)}) copy-start(s32[5,1,128]{2,1,0:T(1,128)} %param.25) | copy-start | bytes 7684
  2.2 11.6 %copy-start.4 = (s32[5,1,128,1]{2,3,1,0:T(1,128)S(1)}, s32[5,1,128,1]{2,3,1,0:T(1,128)}, u32[]{:S(2)}) copy-start(s32[5,1,128,1]{2,3,1,0:T(1,128)} %param.24) | copy-start | bytes 7684
  2.2 23.5 %copy-start.2 = (f32[8,4096]{1,0:T(8,128)S(1)}, f32[8,4096]{1,0:T(8,128)}, u32[]{:S(2)}) copy-start(f32[8,4096]{1,0:T(8,128)} %param.17) | copy-start | bytes 393220
  2.3 23.5 %copy-start.3 = (f32[8,4096]{1,0:T(8,128)S(1)}, f32[8,4096]{1,0:T(8,128)}, u32[]{:S(2)}) copy-start(f32[8,4096]{1,0:T(8,128)} %param.16) | copy-start | bytes 393220
  2.3 23.6 %copy-start.1 = (f32[8,4096]{1,0:T(8,128)S(1)}, f32[8,4096]{1,0:T(8,128)}, u32[]{:S(2)}) copy-start(f32[8,4096]{1,0:T(8,128)} %param.15) | copy-start | bytes 393220
  2.3 32.8 %copy-start = (f32[4096]{0:T(1024)S(1)}, f32[4096]{0:T(1024)}, u32[]{:S(2)}) copy-start(f32[4096]{0:T(1024)} %param.19) | copy-start | bytes 49156
  2.3 32.8 %copy-start.7 = (f32[4096]{0:T(1024)S(1)}, f32[4096]{0:T(1024)}, u32[]{:S(2)}) copy-start(f32[4096]{0:T(1024)} %param.18) | copy-start | bytes 49156
  2.3 32.8 %copy-start.8 = (s32[32]{0:T(128)S(1)}, s32[32]{0:T(128)}, u32[]{:S(2)}) copy-start(s32[32]{0:T(128)} %param.23) | copy-start | bytes 388
  14.6 20.4 %all-to-all-start.1 = ((s32[5,128,1]{0,2,1:T(1,128)}), s32[5,128,1]{0,2,1:T(1,128)S(1)}, u32[]{:S(2)}, u32[]{:S(2)}) async-start(s32[5,128,1]{0,2,1:T(1,128)} %copy.58), calls=%async_computation.1 | async-start | bytes 131072 | tf_op jit(solution)/shard_map/all_to_all | solution.py:52
  46.7 15.3 %all-to-all-start = ((bf16[128,1,8,128]{3,2,1,0:T(8,128)(2,1)}), bf16[128,1,8,128]{3,2,1,0:T(8,128)(2,1)S(1)}, u32[]{:S(2)}, u32[]{:S(2)}) async-start(bf16[128,1,8,128]{3,2,1,0:T(8,128)(2,1)} %fusion.55), calls=%async_computation | async-start | bytes 524288 | tf_op jit(solution)/shard_map/while/body/eval_jaxpr/all_to_all | solution.py:77
  73.8 15.3 %all-to-all-start = ((bf16[128,1,8,128]{3,2,1,0:T(8,128)(2,1)}), bf16[128,1,8,128]{3,2,1,0:T(8,128)(2,1)S(1)}, u32[]{:S(2)}, u32[]{:S(2)}) async-start(bf16[128,1,8,128]{3,2,1,0:T(8,128)(2,1)} %fusion.55), calls=%async_computation | async-start | bytes 524288 | tf_op jit(solution)/shard_map/while/body/eval_jaxpr/all_to_all | solution.py:77
  100.8 15.3 %all-to-all-start = ((bf16[128,1,8,128]{3,2,1,0:T(8,128)(2,1)}), bf16[128,1,8,128]{3,2,1,0:T(8,128)(2,1)S(1)}, u32[]{:S(2)}, u32[]{:S(2)}) async-start(bf16[128,1,8,128]{3,2,1,0:T(8,128)(2,1)} %fusion.55), calls=%async_computation | async-start | bytes 524288 | tf_op jit(solution)/shard_map/while/body/eval_jaxpr/all_to_all | solution.py:77
  127.9 15.3 %all-to-all-start = ((bf16[128,1,8,128]{3,2,1,0:T(8,128)(2,1)}), bf16[128,1,8,128]{3,2,1,0:T(8,128)(2,1)S(1)}, u32[]{:S(2)}, u32[]{:S(2)}) async-start(bf16[128,1,8,128]{3,2,1,0:T(8,128)(2,1)} %fusion.55), calls=%async_computation | async-start | bytes 524288 | tf_op jit(solution)/shard_map/while/body/eval_jaxpr/all_to_all | solution.py:77
  155.0 15.3 %all-to-all-start = ((bf16[128,1,8,128]{3,2,1,0:T(8,128)(2,1)}), bf16[128,1,8,128]{3,2,1,0:T(8,128)(2,1)S(1)}, u32[]{:S(2)}, u32[]{:S(2)}) async-start(bf16[128,1,8,128]{3,2,1,0:T(8,128)(2,1)} %fusion.55), calls=%async_computation | async-start | bytes 524288 | tf_op jit(solution)/shard_map/while/body/eval_jaxpr/all_to_all | solution.py:77
  171.2 8.5 %all-to-all-start.2 = ((f32[4,1,320]{2,1,0:T(1,128)}), f32[4,1,320]{2,1,0:T(1,128)S(1)}, u32[]{:S(2)}, u32[]{:S(2)}) async-start(f32[4,1,320]{2,1,0:T(1,128)} %reshape.391), calls=%async_computation.2 | async-start | bytes 12288 | tf_op jit(solution)/shard_map/all_to_all | solution.py:14
where the time goes:
time: 182 us
  waiting for transfers between devices  65.1 us (36%)
  local copies, waits for them, and re-layouts  51.9 us (29%)
  starting transfers between devices  37.5 us (21%)
  matrix products  22.6 us (12%)
  other arithmetic  3.01 us (2%)
    all_to_all x5, waiting for transfers between devices, advance(): lax.all_to_all(outgoing, ('area', 'local'), split_axis=0, concat_axis=0,...  52.2 us
    gather x5, local copies, waits for them, and re-layouts, advance(): picked = jnp.take_along_axis(tile_table, chosen[:, :, None, None], axis=1)  32.3 us
    all_to_all x5, starting transfers between devices, advance(): lax.all_to_all(outgoing, ('area', 'local'), split_axis=0, concat_axis=0,...  23.1 us
    dot_general x5, matrix products, advance(): jnp.einsum('tcrn,tcnm->tcrm', senders, picked, preferred_element_type=jnp...  20.8 us
    all_to_all x1, starting transfers between devices, shards(): lax.all_to_all(dst_ids, ('area', 'local'), split_axis=1, concat_axis=1, t...  11.2 us
    all_to_all x1, waiting for transfers between devices, shards(): lax.all_to_all(dst_ids, ('area', 'local'), split_axis=1, concat_axis=1, t...  9.13 us
    gather x2, local copies, waits for them, and re-layouts, shards(): jnp.take_along_axis(jnp.broadcast_to(tile_dst[0][None], table_shape), rou...  5.64 us
    gather x2, local copies, waits for them, and re-layouts, shards(): jnp.take_along_axis(jnp.broadcast_to(tile_src[0][None], table_shape), rou...  5.64 us
  transfers between devices with their start and end apart: 7, of which 7 were waited for; matrix products, arithmetic and copies ran while one was open for 1% of the time, Pallas kernels for 0%

commit v1 on v0

--- a/solution.py
+++ b/solution.py
@@ -49,8 +49,14 @@
         jnp.broadcast_to(tile_dst[0][None], table_shape), routes, axis=2
     )
     dst_ids = jnp.where(slot_valid, dst_blocks, -1)
-    arrived_ids = lax.all_to_all(
-        dst_ids, ("area", "local"), split_axis=1, concat_axis=1, tiled=True
+    arrived_ids = jnp.concatenate(
+        lax.all_to_all(
+            jnp.stack(jnp.split(dst_ids, lax.axis_size(("area", "local")), axis=1)),
+            ("area", "local"),
+            0,
+            0,
+        ),
+        axis=1,
     )
     state_shape = (trial_count, blk_count, block_width)
     volts = potential.reshape(state_shape)

time: 182 us -> 260 us (1.43)
  local copies, waits for them, and re-layouts: 51.9 us -> 130 us
    unnamed x25 -> x151, local copies, waits for them, and re-layouts: 2.42 us -> 67.3 us
    split x0 -> x7, local copies, waits for them, and re-layouts: none -> 13.1 us  [shards(): jnp.split(dst_ids, lax.axis_size(('area', 'local')), axis=1)]
where the time goes in v1:
time: 260 us; the launch traced here: 259 us
  local copies, waits for them, and re-layouts  130 us (50%)
  waiting for transfers between devices  65.1 us (25%)
  starting transfers between devices  37.5 us (14%)
  matrix products  22.6 us (9%)
  other arithmetic  3.01 us (1%)
    unnamed x151, local copies, waits for them, and re-layouts  67.3 us
    all_to_all x5, waiting for transfers between devices, advance(): lax.all_to_all(outgoing, ('area', 'local'), split_axis=0, concat_axis=0,...  52.2 us
    gather x5, local copies, waits for them, and re-layouts, advance(): picked = jnp.take_along_axis(tile_table, chosen[:, :, None, None], axis=1)  32.2 us
    all_to_all x5, starting transfers between devices, advance(): lax.all_to_all(outgoing, ('area', 'local'), split_axis=0, concat_axis=0,...  23.1 us
    dot_general x5, matrix products, advance(): jnp.einsum('tcrn,tcnm->tcrm', senders, picked, preferred_element_type=jnp...  20.7 us
    split x7, local copies, waits for them, and re-layouts, shards(): jnp.split(dst_ids, lax.axis_size(('area', 'local')), axis=1)  13.1 us
    all_to_all x1, starting transfers between devices, shards(): lax.all_to_all(jnp.stack(jnp.split(dst_ids, lax.axis_size(('area', 'local...  11.2 us
    all_to_all x1, waiting for transfers between devices, shards(): lax.all_to_all(jnp.stack(jnp.split(dst_ids, lax.axis_size(('area', 'local...  9.13 us
  transfers between devices with their start and end apart: 7, of which 7 were waited for; matrix products, arithmetic and copies ran while one was open for 1% of the time, Pallas kernels for 0%

profile of v1, /device:TPU:0, one launch (start us, length us, event | category | flops | bytes accessed | tf_op | source)
XLA Modules:
  0.0 259.3 jit_solution(2038321351282050173)
XLA Ops:
  0.6 0.7 fusion.37
  1.4 0.8 copy.584
  2.3 5.6 %gather_fusion.2 = s32[640]{0:T(1024)S(1)} fusion(s32[5,128,2]{2,1,0:T(8,128)S(1)} %broadcast_in_dim.74, s32[640]{0:T(1024)S(1)} %bitcast.376), kind=kCustom, calls=%fused_computation.clone | custom fusion | bytes 12800 | tf_op jit(solution)/shard_map/jit(take_along_axis)/gather | solution.py:45
  8.1 5.6 %gather_fusion.3 = s32[640]{0:T(1024)S(1)} fusion(s32[5,128,2]{2,1,0:T(8,128)S(1)} %broadcast_in_dim.76, s32[640]{0:T(1024)S(1)} %bitcast.377), kind=kCustom, calls=%fused_computation.3.clone | custom fusion | bytes 12800 | tf_op jit(solution)/shard_map/jit(take_along_axis)/gather | solution.py:48
  13.8 1.4 slice_reduce_fusion.114
  15.2 1.9 slice_reduce_fusion.95
  17.2 1.9 slice_reduce_fusion.76
  19.1 1.9 slice_reduce_fusion.57
  21.0 1.9 slice_reduce_fusion.38
  22.9 1.9 slice_reduce_fusion.19
  24.8 2.1 slice_reduce_fusion
  26.9 0.5 constant_dynamic-update-slice_fusion.127
  30.0 0.5 constant_dynamic-update-slice_fusion.121
  30.5 0.5 constant_dynamic-update-slice_fusion.120
  31.0 0.5 constant_dynamic-update-slice_fusion.119
  31.5 0.5 constant_dynamic-update-slice_fusion.118
  32.0 0.5 constant_dynamic-update-slice_fusion.117
  32.5 0.5 constant_dynamic-update-slice_fusion.116
  33.0 0.5 constant_dynamic-update-slice_fusion.115
  33.5 0.5 constant_dynamic-update-slice_fusion.114
  34.1 0.5 constant_dynamic-update-slice_fusion.113
  34.6 0.5 constant_dynamic-update-slice_fusion.112
  35.1 0.5 constant_dynamic-update-slice_fusion.111
  35.6 0.5 constant_dynamic-update-slice_fusion.110
  39.7 0.5 constant_dynamic-update-slice_fusion.102
  40.2 0.5 constant_dynamic-update-slice_fusion.101
  40.7 0.5 constant_dynamic-update-slice_fusion.100
  41.2 0.5 constant_dynamic-update-slice_fusion.99
  41.7 0.5 constant_dynamic-update-slice_fusion.98
  92.4 11.2 %all-to-all-start.1 = ((s32[128,5,1,1]{1,3,2,0:T(1,128)}), s32[128,5,1,1]{1,3,2,0:T(1,128)S(1)}, u32[]{:S(2)}, u32[]{:S(2)}) async-start(s32[128,5,1,1]{1,3,2,0:T(1,128)} %constant_dynamic-update-slice_fusion), calls=%async_computation.1 | async-start | bytes 131072 | tf_op jit(solution)/shard_map/all_to_all | solution.py:53
  103.7 9.1 %all-to-all-done.1 = s32[128,5,1,1]{1,3,2,0:T(1,128)S(1)} async-done(((s32[128,5,1,1]{1,3,2,0:T(1,128)}), s32[128,5,1,1]{1,3,2,0:T(1,128)S(1)}, u32[]{:S(2)}, u32[]{:S(2)}) %all-to-all-start.1) | async-done | bytes 2592 | tf_op jit(solution)/shard_map/all_to_all | solution.py:53
  112.9 135.2 %while.20 = (s32[]{:T(128)}, f32[8,32,128]{2,1,0:T(8,128)S(1)}, f32[8,32,128]{2,1,0:T(8,128)S(1)}, f32[5,8,8]{2,1,0:T(8,128)S(1)}, f32[1,32,128]{2,1,0:T(8,128)S...) while((s32[]{:T(128)}, f32[8,32,128]{2,1,0:T(8,128)S(1)}, ...), condition=%wide.region_2.0_spmd.clone, body=%wide.region_0.3_spmd.clone.sunk | while | flops 44994944 | bytes 15770289 | solution.py:99
  113.2 0.7 gather_fusion.1
  113.9 6.4 %gather_fusion = bf16[128,128,128]{2,1,0:T(8,128)(2,1)} fusion(bf16[128,2,128,128]{3,2,1,0:T(8,128)(2,1)} %get-tuple-element.674, s32[128]{0:T(128)S(1)} %or_bitcast_fusion.2), kind=kCustom, calls=%fused_computation.2.clone.clone.1 | custom fusion | bytes 8389632 | tf_op jit(solution)/shard_map/while/body/eval_jaxpr/jit(take_along_axis)/gather | solution.py:78
  120.3 4.1 %fusion.55 = bf16[128,1,8,128]{3,2,1,0:T(8,128)(2,1)} fusion(bf16[128,128,128]{2,1,0:T(8,128)(2,1)} %gather_fusion, pred[128]{0:T(512)(128)(4,1)S(1)} %get-tuple-element.634, bf16[128,8,128]{2,1,0:T(8,128)(2,1)S(1)} %gather_fusion.1, pred[128]{0:T(512)(128)(4,1)S(1)} %get-tuple-element.636), kind=kOutput, calls=%fused_computation.11.clone.1 | convolution fusion | flops 35913728 | bytes 4718848 | tf_op jit(solution)/shard_map/while/body/eval_jaxpr/tcrn,tcnm->tcrm/dot_general | solution.py:80
  124.5 4.6 %all-to-all-start = ((bf16[128,1,8,128]{3,2,1,0:T(8,128)(2,1)}), bf16[128,1,8,128]{3,2,1,0:T(8,128)(2,1)S(1)}, u32[]{:S(2)}, u32[]{:S(2)}) async-start(bf16[128,1,8,128]{3,2,1,0:T(8,128)(2,1)} %fusion.55), calls=%async_computation | async-start | bytes 524288 | tf_op jit(solution)/shard_map/while/body/eval_jaxpr/all_to_all | solution.py:83
  129.3 10.4 %all-to-all-done = bf16[128,1,8,128]{3,2,1,0:T(8,128)(2,1)S(1)} async-done(((bf16[128,1,8,128]{3,2,1,0:T(8,128)(2,1)}), bf16[128,1,8,128]{3,2,1,0:T(8,128)(2,1)S(1)}, u32[]{:S(2)}, u32[]{:S(2)}) %all-to-all-start) | async-done | bytes 262176 | tf_op jit(solution)/shard_map/while/body/eval_jaxpr/all_to_all | solution.py:83
  140.3 0.7 gather_fusion.1
  140.9 6.4 %gather_fusion = bf16[128,128,128]{2,1,0:T(8,128)(2,1)} fusion(bf16[128,2,128,128]{3,2,1,0:T(8,128)(2,1)} %get-tuple-element.674, s32[128]{0:T(128)S(1)} %or_bitcast_fusion.2), kind=kCustom, calls=%fused_computation.2.clone.clone.1 | custom fusion | bytes 8389632 | tf_op jit(solution)/shard_map/while/body/eval_jaxpr/jit(take_along_axis)/gather | solution.py:78
  147.4 4.1 %fusion.55 = bf16[128,1,8,128]{3,2,1,0:T(8,128)(2,1)} fusion(bf16[128,128,128]{2,1,0:T(8,128)(2,1)} %gather_fusion, pred[128]{0:T(512)(128)(4,1)S(1)} %get-tuple-element.634, bf16[128,8,128]{2,1,0:T(8,128)(2,1)S(1)} %gather_fusion.1, pred[128]{0:T(512)(128)(4,1)S(1)} %get-tuple-element.636), kind=kOutput, calls=%fused_computation.11.clone.1 | convolution fusion | flops 35913728 | bytes 4718848 | tf_op jit(solution)/shard_map/while/body/eval_jaxpr/tcrn,tcnm->tcrm/dot_general | solution.py:80
  151.5 4.6 %all-to-all-start = ((bf16[128,1,8,128]{3,2,1,0:T(8,128)(2,1)}), bf16[128,1,8,128]{3,2,1,0:T(8,128)(2,1)S(1)}, u32[]{:S(2)}, u32[]{:S(2)}) async-start(bf16[128,1,8,128]{3,2,1,0:T(8,128)(2,1)} %fusion.55), calls=%async_computation | async-start | bytes 524288 | tf_op jit(solution)/shard_map/while/body/eval_jaxpr/all_to_all | solution.py:83
  156.4 10.4 %all-to-all-done = bf16[128,1,8,128]{3,2,1,0:T(8,128)(2,1)S(1)} async-done(((bf16[128,1,8,128]{3,2,1,0:T(8,128)(2,1)}), bf16[128,1,8,128]{3,2,1,0:T(8,128)(2,1)S(1)}, u32[]{:S(2)}, u32[]{:S(2)}) %all-to-all-start) | async-done | bytes 262176 | tf_op jit(solution)/shard_map/while/body/eval_jaxpr/all_to_all | solution.py:83
  167.3 0.7 gather_fusion.1
  168.0 6.4 %gather_fusion = bf16[128,128,128]{2,1,0:T(8,128)(2,1)} fusion(bf16[128,2,128,128]{3,2,1,0:T(8,128)(2,1)} %get-tuple-element.674, s32[128]{0:T(128)S(1)} %or_bitcast_fusion.2), kind=kCustom, calls=%fused_computation.2.clone.clone.1 | custom fusion | bytes 8389632 | tf_op jit(solution)/shard_map/while/body/eval_jaxpr/jit(take_along_axis)/gather | solution.py:78
  174.4 4.1 %fusion.55 = bf16[128,1,8,128]{3,2,1,0:T(8,128)(2,1)} fusion(bf16[128,128,128]{2,1,0:T(8,128)(2,1)} %gather_fusion, pred[128]{0:T(512)(128)(4,1)S(1)} %get-tuple-element.634, bf16[128,8,128]{2,1,0:T(8,128)(2,1)S(1)} %gather_fusion.1, pred[128]{0:T(512)(128)(4,1)S(1)} %get-tuple-element.636), kind=kOutput, calls=%fused_computation.11.clone.1 | convolution fusion | flops 35913728 | bytes 4718848 | tf_op jit(solution)/shard_map/while/body/eval_jaxpr/tcrn,tcnm->tcrm/dot_general | solution.py:80
  178.6 4.6 %all-to-all-start = ((bf16[128,1,8,128]{3,2,1,0:T(8,128)(2,1)}), bf16[128,1,8,128]{3,2,1,0:T(8,128)(2,1)S(1)}, u32[]{:S(2)}, u32[]{:S(2)}) async-start(bf16[128,1,8,128]{3,2,1,0:T(8,128)(2,1)} %fusion.55), calls=%async_computation | async-start | bytes 524288 | tf_op jit(solution)/shard_map/while/body/eval_jaxpr/all_to_all | solution.py:83
  183.4 10.4 %all-to-all-done = bf16[128,1,8,128]{3,2,1,0:T(8,128)(2,1)S(1)} async-done(((bf16[128,1,8,128]{3,2,1,0:T(8,128)(2,1)}), bf16[128,1,8,128]{3,2,1,0:T(8,128)(2,1)S(1)}, u32[]{:S(2)}, u32[]{:S(2)}) %all-to-all-start) | async-done | bytes 262176 | tf_op jit(solution)/shard_map/while/body/eval_jaxpr/all_to_all | solution.py:83
  194.3 0.7 gather_fusion.1
  195.0 6.4 %gather_fusion = bf16[128,128,128]{2,1,0:T(8,128)(2,1)} fusion(bf16[128,2,128,128]{3,2,1,0:T(8,128)(2,1)} %get-tuple-element.674, s32[128]{0:T(128)S(1)} %or_bitcast_fusion.2), kind=kCustom, calls=%fused_computation.2.clone.clone.1 | custom fusion | bytes 8389632 | tf_op jit(solution)/shard_map/while/body/eval_jaxpr/jit(take_along_axis)/gather | solution.py:78
  201.4 4.1 %fusion.55 = bf16[128,1,8,128]{3,2,1,0:T(8,128)(2,1)} fusion(bf16[128,128,128]{2,1,0:T(8,128)(2,1)} %gather_fusion, pred[128]{0:T(512)(128)(4,1)S(1)} %get-tuple-element.634, bf16[128,8,128]{2,1,0:T(8,128)(2,1)S(1)} %gather_fusion.1, pred[128]{0:T(512)(128)(4,1)S(1)} %get-tuple-element.636), kind=kOutput, calls=%fused_computation.11.clone.1 | convolution fusion | flops 35913728 | bytes 4718848 | tf_op jit(solution)/shard_map/while/body/eval_jaxpr/tcrn,tcnm->tcrm/dot_general | solution.py:80
  205.6 4.6 %all-to-all-start = ((bf16[128,1,8,128]{3,2,1,0:T(8,128)(2,1)}), bf16[128,1,8,128]{3,2,1,0:T(8,128)(2,1)S(1)}, u32[]{:S(2)}, u32[]{:S(2)}) async-start(bf16[128,1,8,128]{3,2,1,0:T(8,128)(2,1)} %fusion.55), calls=%async_computation | async-start | bytes 524288 | tf_op jit(solution)/shard_map/while/body/eval_jaxpr/all_to_all | solution.py:83
  210.4 10.4 %all-to-all-done = bf16[128,1,8,128]{3,2,1,0:T(8,128)(2,1)S(1)} async-done(((bf16[128,1,8,128]{3,2,1,0:T(8,128)(2,1)}), bf16[128,1,8,128]{3,2,1,0:T(8,128)(2,1)S(1)}, u32[]{:S(2)}, u32[]{:S(2)}) %all-to-all-start) | async-done | bytes 262176 | tf_op jit(solution)/shard_map/while/body/eval_jaxpr/all_to_all | solution.py:83
  221.3 0.7 gather_fusion.1
  222.0 6.4 %gather_fusion = bf16[128,128,128]{2,1,0:T(8,128)(2,1)} fusion(bf16[128,2,128,128]{3,2,1,0:T(8,128)(2,1)} %get-tuple-element.674, s32[128]{0:T(128)S(1)} %or_bitcast_fusion.2), kind=kCustom, calls=%fused_computation.2.clone.clone.1 | custom fusion | bytes 8389632 | tf_op jit(solution)/shard_map/while/body/eval_jaxpr/jit(take_along_axis)/gather | solution.py:78
  228.5 4.1 %fusion.55 = bf16[128,1,8,128]{3,2,1,0:T(8,128)(2,1)} fusion(bf16[128,128,128]{2,1,0:T(8,128)(2,1)} %gather_fusion, pred[128]{0:T(512)(128)(4,1)S(1)} %get-tuple-element.634, bf16[128,8,128]{2,1,0:T(8,128)(2,1)S(1)} %gather_fusion.1, pred[128]{0:T(512)(128)(4,1)S(1)} %get-tuple-element.636), kind=kOutput, calls=%fused_computation.11.clone.1 | convolution fusion | flops 35913728 | bytes 4718848 | tf_op jit(solution)/shard_map/while/body/eval_jaxpr/tcrn,tcnm->tcrm/dot_general | solution.py:80
  232.6 4.6 %all-to-all-start = ((bf16[128,1,8,128]{3,2,1,0:T(8,128)(2,1)}), bf16[128,1,8,128]{3,2,1,0:T(8,128)(2,1)S(1)}, u32[]{:S(2)}, u32[]{:S(2)}) async-start(bf16[128,1,8,128]{3,2,1,0:T(8,128)(2,1)} %fusion.55), calls=%async_computation | async-start | bytes 524288 | tf_op jit(solution)/shard_map/while/body/eval_jaxpr/all_to_all | solution.py:83
  237.5 10.4 %all-to-all-done = bf16[128,1,8,128]{3,2,1,0:T(8,128)(2,1)S(1)} async-done(((bf16[128,1,8,128]{3,2,1,0:T(8,128)(2,1)}), bf16[128,1,8,128]{3,2,1,0:T(8,128)(2,1)S(1)}, u32[]{:S(2)}, u32[]{:S(2)}) %all-to-all-start) | async-done | bytes 262176 | tf_op jit(solution)/shard_map/while/body/eval_jaxpr/all_to_all | solution.py:83
  248.1 0.7 reshape.527
  248.8 3.2 %all-to-all-start.2 = ((f32[4,1,320]{2,1,0:T(1,128)}), f32[4,1,320]{2,1,0:T(1,128)S(1)}, u32[]{:S(2)}, u32[]{:S(2)}) async-start(f32[4,1,320]{2,1,0:T(1,128)} %reshape.527), calls=%async_computation.2 | async-start | bytes 12288 | tf_op jit(solution)/shard_map/all_to_all | solution.py:14
  252.1 0.7 copy.611
  252.8 0.7 copy.612
  253.5 3.8 %all-to-all-done.2 = f32[4,1,320]{2,1,0:T(1,128)S(1)} async-done(((f32[4,1,320]{2,1,0:T(1,128)}), f32[4,1,320]{2,1,0:T(1,128)S(1)}, u32[]{:S(2)}, u32[]{:S(2)}) %all-to-all-start.2) | async-done | bytes 5152 | tf_op jit(solution)/shard_map/all_to_all | solution.py:14
  257.8 0.7 reduce.258
  258.6 0.6 multiply_bitcast_fusion
  (213 shorter events, 60.3 us)
Async XLA Ops:
  0.6 7.3 %copy-start.6 = (s32[1,128,2]{1,2,0:T(2,128)S(1)}, s32[1,128,2]{1,2,0:T(2,128)}, u32[]{:S(2)}) copy-start(s32[1,128,2]{1,2,0:T(2,128)} %param.22) | copy-start | bytes 3076
  2.2 11.5 %copy-start.5 = (s32[5,1,128]{2,1,0:T(1,128)S(1)}, s32[5,1,128]{2,1,0:T(1,128)}, u32[]{:S(2)}) copy-start(s32[5,1,128]{2,1,0:T(1,128)} %param.25) | copy-start | bytes 7684
  2.2 11.6 %copy-start.4 = (s32[5,1,128,1]{2,3,1,0:T(1,128)S(1)}, s32[5,1,128,1]{2,3,1,0:T(1,128)}, u32[]{:S(2)}) copy-start(s32[5,1,128,1]{2,3,1,0:T(1,128)} %param.24) | copy-start | bytes 7684
  2.2 101.3 %copy-start.2 = (f32[8,4096]{1,0:T(8,128)S(1)}, f32[8,4096]{1,0:T(8,128)}, u32[]{:S(2)}) copy-start(f32[8,4096]{1,0:T(8,128)} %param.17) | copy-start | bytes 393220
  2.3 101.3 %copy-start.3 = (f32[8,4096]{1,0:T(8,128)S(1)}, f32[8,4096]{1,0:T(8,128)}, u32[]{:S(2)}) copy-start(f32[8,4096]{1,0:T(8,128)} %param.16) | copy-start | bytes 393220
  7.9 95.7 %copy-start.1 = (f32[8,4096]{1,0:T(8,128)S(1)}, f32[8,4096]{1,0:T(8,128)}, u32[]{:S(2)}) copy-start(f32[8,4096]{1,0:T(8,128)} %param.15) | copy-start | bytes 393220
  7.9 105.0 %copy-start = (f32[4096]{0:T(1024)S(1)}, f32[4096]{0:T(1024)}, u32[]{:S(2)}) copy-start(f32[4096]{0:T(1024)} %param.19) | copy-start | bytes 49156
  7.9 105.0 %copy-start.7 = (f32[4096]{0:T(1024)S(1)}, f32[4096]{0:T(1024)}, u32[]{:S(2)}) copy-start(f32[4096]{0:T(1024)} %param.18) | copy-start | bytes 49156
  7.9 105.0 %copy-start.8 = (s32[32]{0:T(128)S(1)}, s32[32]{0:T(128)}, u32[]{:S(2)}) copy-start(s32[32]{0:T(128)} %param.23) | copy-start | bytes 388
  92.4 20.4 %all-to-all-start.1 = ((s32[128,5,1,1]{1,3,2,0:T(1,128)}), s32[128,5,1,1]{1,3,2,0:T(1,128)S(1)}, u32[]{:S(2)}, u32[]{:S(2)}) async-start(s32[128,5,1,1]{1,3,2,0:T(1,128)} %constant_dynamic-update-slice_fusion), calls=%async_computation.1 | async-start | bytes 131072 | tf_op jit(solution)/shard_map/all_to_all | solution.py:53
  124.5 15.3 %all-to-all-start = ((bf16[128,1,8,128]{3,2,1,0:T(8,128)(2,1)}), bf16[128,1,8,128]{3,2,1,0:T(8,128)(2,1)S(1)}, u32[]{:S(2)}, u32[]{:S(2)}) async-start(bf16[128,1,8,128]{3,2,1,0:T(8,128)(2,1)} %fusion.55), calls=%async_computation | async-start | bytes 524288 | tf_op jit(solution)/shard_map/while/body/eval_jaxpr/all_to_all | solution.py:83
  151.5 15.3 %all-to-all-start = ((bf16[128,1,8,128]{3,2,1,0:T(8,128)(2,1)}), bf16[128,1,8,128]{3,2,1,0:T(8,128)(2,1)S(1)}, u32[]{:S(2)}, u32[]{:S(2)}) async-start(bf16[128,1,8,128]{3,2,1,0:T(8,128)(2,1)} %fusion.55), calls=%async_computation | async-start | bytes 524288 | tf_op jit(solution)/shard_map/while/body/eval_jaxpr/all_to_all | solution.py:83
  178.6 15.3 %all-to-all-start = ((bf16[128,1,8,128]{3,2,1,0:T(8,128)(2,1)}), bf16[128,1,8,128]{3,2,1,0:T(8,128)(2,1)S(1)}, u32[]{:S(2)}, u32[]{:S(2)}) async-start(bf16[128,1,8,128]{3,2,1,0:T(8,128)(2,1)} %fusion.55), calls=%async_computation | async-start | bytes 524288 | tf_op jit(solution)/shard_map/while/body/eval_jaxpr/all_to_all | solution.py:83
  205.6 15.3 %all-to-all-start = ((bf16[128,1,8,128]{3,2,1,0:T(8,128)(2,1)}), bf16[128,1,8,128]{3,2,1,0:T(8,128)(2,1)S(1)}, u32[]{:S(2)}, u32[]{:S(2)}) async-start(bf16[128,1,8,128]{3,2,1,0:T(8,128)(2,1)} %fusion.55), calls=%async_computation | async-start | bytes 524288 | tf_op jit(solution)/shard_map/while/body/eval_jaxpr/all_to_all | solution.py:83
  232.6 15.3 %all-to-all-start = ((bf16[128,1,8,128]{3,2,1,0:T(8,128)(2,1)}), bf16[128,1,8,128]{3,2,1,0:T(8,128)(2,1)S(1)}, u32[]{:S(2)}, u32[]{:S(2)}) async-start(bf16[128,1,8,128]{3,2,1,0:T(8,128)(2,1)} %fusion.55), calls=%async_computation | async-start | bytes 524288 | tf_op jit(solution)/shard_map/while/body/eval_jaxpr/all_to_all | solution.py:83
  248.8 8.5 %all-to-all-start.2 = ((f32[4,1,320]{2,1,0:T(1,128)}), f32[4,1,320]{2,1,0:T(1,128)S(1)}, u32[]{:S(2)}, u32[]{:S(2)}) async-start(f32[4,1,320]{2,1,0:T(1,128)} %reshape.527), calls=%async_computation.2 | async-start | bytes 12288 | tf_op jit(solution)/shard_map/all_to_all | solution.py:14
